TPU v7x, 32 devices: a whole 2x2x4 slice. The times are simulated.
32 devices in a mesh: row: 8 (over z, x), col: 4 (over y, core).
Axes of the slice: x: 2, y: 2, z: 4, core: 2. Of those that a mesh axis runs over, the one named last changes fastest.
Arguments:
- positions: float32 [3, 24576], P(None, ('row', 'col')), may hold values from -0.5 to 209.5, as said below
- widths: float32 [24576], P(('row', 'col')), may hold values from 0.8 to 1.6
- hardness: float32 [24576], P(('row', 'col')), may hold values from 16 to 48
- right_sides: float32 [64, 24576], P(None, ('row', 'col')), may hold values from -700 to 700
Outputs:
- charges: float32 [64, 24576], P(None, ('row', 'col'))
- residual: float32 [64, 24576], P(None, ('row', 'col'))
Inputs may be any that keep to these rules, and one draw needn't show every extreme that they name: `positions`: atoms sit near distinct sites of a lattice of spacing 2.2; any two atoms are 1.2 or more apart.
All inputs are finite; a program needn't handle non-finite values.
Results may differ from a plain program's by a relative error of at most 0.0003.
Values sent between devices are 32-bit elements; how exact they have to be, the bound alone decides.
No kernel may reach another device: no remote copies, remote signals or barrier semaphores. Data moves between devices by JAX's collectives and lax.ppermute only.
A program may use at most 128 MiB of HBM per device.

v0:
```python
import jax
import jax.numpy as jnp
from jax import lax
from jax.sharding import PartitionSpec as P

ITERS = 6
root_two = 1.4142135623730951
sqrt_pi = 1.7724538509055159


def kernel_block(pos_a, wid_a, pos_b, wid_b):
    squared = jnp.zeros((pos_a.shape[1], pos_b.shape[1]), jnp.float32)
    for axis_id in range(3):
        delta = pos_a[axis_id][:, None] - pos_b[axis_id][None, :]
        squared = squared + delta * delta
    distinct = squared > 0.25
    distance = jnp.sqrt(jnp.maximum(squared, 0.25))
    width_pair = jnp.sqrt(wid_a[:, None] * wid_a[:, None] + wid_b[None, :] * wid_b[None, :])
    coulomb = lax.erf(distance / (root_two * width_pair)) / distance
    return jnp.where(distinct, coulomb, 0.0)


def squared_norm(residual):
    return lax.psum(jnp.sum(residual * residual, axis=1), ("row", "col"))


def local(positions, widths, hardness, right_sides):
    diagonal = hardness + 1.0 / (widths * sqrt_pi)
    all_pos, all_wid = (
        lax.all_gather(positions, ("row", "col"), axis=1, tiled=True),
        lax.all_gather(widths, ("row", "col"), axis=0, tiled=True),
    )
    coupling = kernel_block(positions, widths, all_pos, all_wid)
    charges = jnp.zeros_like(right_sides)
    residual = right_sides
    search = right_sides
    norm_now = squared_norm(residual)
    for iteration in range(ITERS):
        summed = lax.dot_general(
            lax.all_gather(search, ("row", "col"), axis=1, tiled=True),
            coupling,
            (((1,), (1,)), ((), ())),
            precision=lax.Precision.HIGHEST,
            preferred_element_type=jnp.float32,
        )
        mapped = summed + diagonal[None, :] * search
        bending = lax.psum(jnp.sum(search * mapped, axis=1), ("row", "col"))
        step_len = norm_now / bending
        charges = charges + step_len[:, None] * search
        residual = residual - step_len[:, None] * mapped
        norm_next = squared_norm(residual)
        search = residual + (norm_next / norm_now)[:, None] * search
        norm_now = norm_next
    return (charges, residual)


def solution(mesh):
    in_specs = (
        P(None, ("row", "col")),
        P(("row", "col")),
        P(("row", "col")),
        P(None, ("row", "col")),
    )
    out_specs = (P(None, ("row", "col")), P(None, ("row", "col")))
    return jax.shard_map(local, mesh=mesh, in_specs=in_specs, out_specs=out_specs, check_vma=False)
```

profile of v0, /device:TPU:0, one launch (start us, length us, event | category | flops | bytes accessed | tf_op | source)
XLA Modules:
  0.0 1521.0 jit_solution(16570144204340177374)
XLA Ops:
  7.2 0.0 copy-start
  7.2 0.0 all-gather.8.cloned.1.call-start
  7.2 0.7 all-gather.8.cloned.1.call-update
  7.9 0.0 all-gather.10.cloned.1.call-start
  8.0 44.8 %all_gather.24 = f32[3,24576]{1,0:T(4,128)S(1)} all-gather(f32[3,768]{1,0:T(4,128)} %param.4), channel_id=1, replica_groups=mesh['row'=8,'col'=4] {'row','col'}, dimensions={1}, use_global_device_ids=true | all-gather | bytes 304128 | tf_op jit(solution)/shard_map/all_gather | solution.py:30
  52.8 0.8 slice_reduce_fusion.2
  53.6 0.2 fusion.53
  53.9 0.7 reshape.23
  54.5 0.7 divide_add_fusion
  55.3 37.7 %all-gather = f32[32,1,768]{2,1,0:T(1,128)S(1)} all-gather(f32[1,1,768]{2,1,0:T(1,128)S(1)} %reshape.23), channel_id=1, replica_groups=mesh['row'=8,'col'=4] {'row','col'}, dimensions={0}, use_global_device_ids=true | all-gather | bytes 101376 | tf_op jit(solution)/shard_map/all_gather | solution.py:31
  93.0 0.1 mul.283
  93.1 82.4 %fusion.19.clone.4 = f32[768,24576]{1,0:T(8,128)} fusion(f32[24576]{0:T(1024)S(1)} %bitcast.40, f32[768]{0:T(1024)S(1)} %get-tuple-element.21, f32[24576]{0:T(1024)S(1)} %bitcast.28, f32[768]{0:T(1024)S(1)} %get-tuple-element.5, f32[24576]{0:T(1024)S(1)} %bitcast.34, f32[768]{0:T(1024)S(1)} %get-tuple-element.6, ...), kind=kLoop, calls=%fused_computation.1.clone.5.clone.clone.clone.clone.clone.clone.clone.1 | loop fusion | flops 283115520 | bytes 75902976 | tf_op jit(solution)/shard_map/reduce_sum | solution.py:47
  175.5 0.0 copy-done
  175.5 78.1 %multiply_reduce_fusion.10 = (f32[64]{0:T(128)S(1)}, f32[64]{0:T(128)S(1)}, f32[64,768]{1,0:T(8,128)S(1)}) fusion(f32[64,768]{1,0:T(8,128)S(1)} %copy-done, f32[768]{0:T(1024)S(1)} %get-tuple-element.20, f32[64,24576]{1,0:T(8,128)} %all-gather.8.cloned.1.call-done, f32[768,24576]{1,0:T(8,128)} %fusion.19.clone.4), kind=kOutput, calls=%fused_computation.39 | convolution fusion | flops 14495809536 | bytes 82185728 | tf_op jit(solution)/shard_map/dot_general | solution.py:39
  253.7 37.1 %all-reduce = (f32[64]{0:T(128)S(1)}, f32[64]{0:T(128)S(1)}) all-reduce(f32[64]{0:T(128)S(1)} %get-tuple-element.3, f32[64]{0:T(128)S(1)} %get-tuple-element.2), channel_id=1, replica_groups=mesh['row'=8,'col'=4] {'row','col'}, use_global_device_ids=true, to_apply=%region_1.2 | all-reduce | flops 128 | bytes 1024 | tf_op jit(solution)/shard_map/psum | solution.py:24
  290.8 0.2 multiply_reduce_fusion.9
  291.0 42.4 %psum.86 = f32[64]{0:T(128)S(1)} all-reduce(f32[64]{0:T(128)S(1)} %multiply_reduce_fusion.9), channel_id=1, replica_groups=mesh['row'=8,'col'=4] {'row','col'}, use_global_device_ids=true, to_apply=%region_5.6 | all-reduce | flops 64 | bytes 512 | tf_op jit(solution)/shard_map/psum | solution.py:24
  333.3 0.8 multiply_add_fusion.6
  334.1 0.0 all-gather.10.cloned.1.call-update
  334.1 0.0 all-gather.12.cloned.1.call-start
  334.2 82.4 %fusion.22.clone.2 = f32[768,24576]{1,0:T(8,128)} fusion(f32[24576]{0:T(1024)S(1)} %bitcast.41, f32[768]{0:T(1024)S(1)} %get-tuple-element.21, f32[24576]{0:T(1024)S(1)} %bitcast.29, f32[768]{0:T(1024)S(1)} %get-tuple-element.5, f32[24576]{0:T(1024)S(1)} %bitcast.35, f32[768]{0:T(1024)S(1)} %get-tuple-element.6, ...), kind=kLoop, calls=%fused_computation.1.clone.4.clone.clone.clone.clone.clone | loop fusion | flops 283115520 | bytes 75902976 | tf_op jit(solution)/shard_map/reduce_sum | solution.py:47
  416.6 0.0 copy-done.2
  416.6 78.3 %multiply_reduce_fusion.8 = (f32[64]{0:T(128)S(1)}, f32[64,768]{1,0:T(8,128)S(1)}) fusion(f32[64,768]{1,0:T(8,128)S(1)} %copy-done.2, f32[768]{0:T(1024)S(1)} %get-tuple-element.20, f32[64,24576]{1,0:T(8,128)} %all-gather.10.cloned.1.call-done, f32[768,24576]{1,0:T(8,128)} %fusion.22.clone.2), kind=kOutput, calls=%fused_computation.35 | convolution fusion | flops 14495711232 | bytes 82185472 | tf_op jit(solution)/shard_map/dot_general | solution.py:39
  494.9 38.3 %psum.87 = f32[64]{0:T(128)S(1)} all-reduce(f32[64]{0:T(128)S(1)} %get-tuple-element.25), channel_id=1, replica_groups=mesh['row'=8,'col'=4] {'row','col'}, use_global_device_ids=true, to_apply=%region_7.8 | all-reduce | flops 64 | bytes 512 | tf_op jit(solution)/shard_map/psum | solution.py:47
  533.3 0.0 copy-done.9
  533.3 0.2 multiply_reduce_fusion.7
  533.5 41.6 %psum.88 = f32[64]{0:T(128)S(1)} all-reduce(f32[64]{0:T(128)S(1)} %get-tuple-element.15), channel_id=1, replica_groups=mesh['row'=8,'col'=4] {'row','col'}, use_global_device_ids=true, to_apply=%region_9.10 | all-reduce | flops 64 | bytes 512 | tf_op jit(solution)/shard_map/psum | solution.py:24
  575.1 0.8 multiply_add_fusion.5
  575.9 0.0 all-gather.12.cloned.1.call-update
  575.9 0.0 all-gather.14.cloned.1.call-start
  575.9 93.9 %fusion.25.clone.2 = f32[768,24576]{1,0:T(8,128)} fusion(f32[24576]{0:T(1024)S(1)} %bitcast.42, f32[768]{0:T(1024)S(1)} %get-tuple-element.21, f32[24576]{0:T(1024)S(1)} %bitcast.30, f32[768]{0:T(1024)S(1)} %get-tuple-element.5, f32[24576]{0:T(1024)S(1)} %bitcast.36, f32[768]{0:T(1024)S(1)} %get-tuple-element.6, ...), kind=kLoop, calls=%fused_computation.1.clone.3.clone.clone.clone.clone.clone | loop fusion | flops 283115520 | bytes 75902976 | tf_op jit(solution)/shard_map/reduce_sum | solution.py:47
  669.8 0.0 copy-done.4
  669.8 78.3 %multiply_reduce_fusion.6 = (f32[64]{0:T(128)S(1)}, f32[64,768]{1,0:T(8,128)S(1)}) fusion(f32[64,768]{1,0:T(8,128)S(1)} %copy-done.4, f32[768]{0:T(1024)S(1)} %get-tuple-element.20, f32[64,24576]{1,0:T(8,128)} %all-gather.12.cloned.1.call-done, f32[768,24576]{1,0:T(8,128)} %fusion.25.clone.2), kind=kOutput, calls=%fused_computation.31 | convolution fusion | flops 14495711232 | bytes 82185472 | tf_op jit(solution)/shard_map/dot_general | solution.py:39
  748.1 0.0 copy-done.13
  748.1 38.4 %psum.89 = f32[64]{0:T(128)S(1)} all-reduce(f32[64]{0:T(128)S(1)} %get-tuple-element.27), channel_id=1, replica_groups=mesh['row'=8,'col'=4] {'row','col'}, use_global_device_ids=true, to_apply=%region_11.12 | all-reduce | flops 64 | bytes 512 | tf_op jit(solution)/shard_map/psum | solution.py:47
  786.5 0.2 multiply_reduce_fusion.5
  786.7 41.5 %psum.90 = f32[64]{0:T(128)S(1)} all-reduce(f32[64]{0:T(128)S(1)} %get-tuple-element.13), channel_id=1, replica_groups=mesh['row'=8,'col'=4] {'row','col'}, use_global_device_ids=true, to_apply=%region_13.14 | all-reduce | flops 64 | bytes 512 | tf_op jit(solution)/shard_map/psum | solution.py:24
  828.2 0.8 multiply_add_fusion.4
  829.0 0.0 all-gather.14.cloned.1.call-update
  829.0 0.0 all-gather.16.cloned.1.call-start
  829.1 82.8 %fusion.28.clone.2 = f32[768,24576]{1,0:T(8,128)} fusion(f32[24576]{0:T(1024)S(1)} %bitcast.43, f32[768]{0:T(1024)S(1)} %get-tuple-element.21, f32[24576]{0:T(1024)S(1)} %bitcast.31, f32[768]{0:T(1024)S(1)} %get-tuple-element.5, f32[24576]{0:T(1024)S(1)} %bitcast.37, f32[768]{0:T(1024)S(1)} %get-tuple-element.6, ...), kind=kLoop, calls=%fused_computation.1.clone.2.clone.clone.clone.clone.clone | loop fusion | flops 283115520 | bytes 75902976 | tf_op jit(solution)/shard_map/reduce_sum | solution.py:47
  911.9 78.3 %multiply_reduce_fusion.4 = (f32[64]{0:T(128)S(1)}, f32[64,768]{1,0:T(8,128)S(1)}) fusion(f32[64,768]{1,0:T(8,128)S(1)} %copy-done.6, f32[768]{0:T(1024)S(1)} %get-tuple-element.20, f32[64,24576]{1,0:T(8,128)} %all-gather.14.cloned.1.call-done, f32[768,24576]{1,0:T(8,128)} %fusion.28.clone.2), kind=kOutput, calls=%fused_computation.27 | convolution fusion | flops 14495711232 | bytes 82185472 | tf_op jit(solution)/shard_map/dot_general | solution.py:39
  990.2 38.5 %psum.91 = f32[64]{0:T(128)S(1)} all-reduce(f32[64]{0:T(128)S(1)} %get-tuple-element.29), channel_id=1, replica_groups=mesh['row'=8,'col'=4] {'row','col'}, use_global_device_ids=true, to_apply=%region_15.16 | all-reduce | flops 64 | bytes 512 | tf_op jit(solution)/shard_map/psum | solution.py:47
  1028.7 0.2 multiply_reduce_fusion.3
  1028.9 41.5 %psum.92 = f32[64]{0:T(128)S(1)} all-reduce(f32[64]{0:T(128)S(1)} %get-tuple-element.11), channel_id=1, replica_groups=mesh['row'=8,'col'=4] {'row','col'}, use_global_device_ids=true, to_apply=%region_17.18 | all-reduce | flops 64 | bytes 512 | tf_op jit(solution)/shard_map/psum | solution.py:24
  1070.4 0.8 multiply_add_fusion.3
  1071.2 0.0 all-gather.16.cloned.1.call-update
  1071.2 0.0 all-gather.18.cloned.1.call-start
  1071.2 82.6 %fusion.31.clone.2 = f32[768,24576]{1,0:T(8,128)} fusion(f32[24576]{0:T(1024)S(1)} %bitcast.44, f32[768]{0:T(1024)S(1)} %get-tuple-element.21, f32[24576]{0:T(1024)S(1)} %bitcast.32, f32[768]{0:T(1024)S(1)} %get-tuple-element.5, f32[24576]{0:T(1024)S(1)} %bitcast.38, f32[768]{0:T(1024)S(1)} %get-tuple-element.6, ...), kind=kLoop, calls=%fused_computation.1.clone.1.clone.clone.clone.clone.clone | loop fusion | flops 283115520 | bytes 75902976 | tf_op jit(solution)/shard_map/reduce_sum | solution.py:47
  1153.8 78.3 %multiply_reduce_fusion.2 = (f32[64]{0:T(128)S(1)}, f32[64,768]{1,0:T(8,128)S(1)}) fusion(f32[64,768]{1,0:T(8,128)S(1)} %copy-done.7, f32[768]{0:T(1024)S(1)} %get-tuple-element.20, f32[64,24576]{1,0:T(8,128)} %all-gather.16.cloned.1.call-done, f32[768,24576]{1,0:T(8,128)} %fusion.31.clone.2), kind=kOutput, calls=%fused_computation.23 | convolution fusion | flops 14495711232 | bytes 82185472 | tf_op jit(solution)/shard_map/dot_general | solution.py:39
  1232.1 38.6 %psum.93 = f32[64]{0:T(128)S(1)} all-reduce(f32[64]{0:T(128)S(1)} %get-tuple-element.31), channel_id=1, replica_groups=mesh['row'=8,'col'=4] {'row','col'}, use_global_device_ids=true, to_apply=%region_19.20 | all-reduce | flops 64 | bytes 512 | tf_op jit(solution)/shard_map/psum | solution.py:47
  1270.7 0.2 multiply_reduce_fusion.1
  1270.9 41.6 %psum.94 = f32[64]{0:T(128)S(1)} all-reduce(f32[64]{0:T(128)S(1)} %get-tuple-element.9), channel_id=1, replica_groups=mesh['row'=8,'col'=4] {'row','col'}, use_global_device_ids=true, to_apply=%region_21.22 | all-reduce | flops 64 | bytes 512 | tf_op jit(solution)/shard_map/psum | solution.py:24
  1312.5 0.8 multiply_add_fusion.2
  1313.3 0.0 all-gather.18.cloned.1.call-update
  1313.3 82.4 %fusion.34.clone.4 = f32[768,24576]{1,0:T(8,128)} fusion(f32[24576]{0:T(1024)S(1)} %bitcast.45, f32[768]{0:T(1024)S(1)} %get-tuple-element.21, f32[24576]{0:T(1024)S(1)} %bitcast.33, f32[768]{0:T(1024)S(1)} %get-tuple-element.5, f32[24576]{0:T(1024)S(1)} %bitcast.39, f32[768]{0:T(1024)S(1)} %get-tuple-element.6, ...), kind=kLoop, calls=%fused_computation.1.clone.clone.clone.clone.clone.clone.1 | loop fusion | flops 283115520 | bytes 75902976 | tf_op jit(solution)/shard_map/reduce_sum | solution.py:47
  1395.7 0.0 copy-start.10
  1395.7 0.0 copy-start.12
  1395.8 0.0 copy-start.14
  1395.8 0.0 all-gather.18.cloned.1.call-done
  1395.8 78.4 %multiply_reduce_fusion = (f32[64]{0:T(128)S(1)}, f32[64,768]{1,0:T(8,128)S(1)}) fusion(f32[64,768]{1,0:T(8,128)S(1)} %copy-done.8, f32[768]{0:T(1024)S(1)} %get-tuple-element.20, f32[64,24576]{1,0:T(8,128)} %all-gather.18.cloned.1.call-done, f32[768,24576]{1,0:T(8,128)} %fusion.34.clone.4), kind=kOutput, calls=%fused_computation.19 | convolution fusion | flops 14495711232 | bytes 82185472 | tf_op jit(solution)/shard_map/dot_general | solution.py:39
  1474.2 38.7 %psum.95 = f32[64]{0:T(128)S(1)} all-reduce(f32[64]{0:T(128)S(1)} %get-tuple-element.33), channel_id=1, replica_groups=mesh['row'=8,'col'=4] {'row','col'}, use_global_device_ids=true, to_apply=%region_23.24 | all-reduce | flops 64 | bytes 512 | tf_op jit(solution)/shard_map/psum | solution.py:47
  1512.8 0.0 copy-done.3
  1512.9 0.9 multiply_subtract_fusion
  (36 shorter events, 0.1 us)
Async XLA Ops:
  7.2 168.3 %copy-start = (f32[64,768]{1,0:T(8,128)S(1)}, f32[64,768]{1,0:T(8,128)}, u32[]{:S(2)}) copy-start(f32[64,768]{1,0:T(8,128)} %param.7) | copy-start | bytes 589828
  7.2 168.3 %all-gather.8.cloned.1.call-start = ((), (), s32[]{:S(2)}) async-start(), calls=%async_computation | async-start | bytes 6488064 | tf_op jit(solution)/shard_map/all_gather | solution.py:40
  7.9 408.7 %all-gather.10.cloned.1.call-start = ((), (), s32[]{:S(2)}) async-start(), calls=%async_computation.1 | async-start | bytes 6488064 | tf_op jit(solution)/shard_map/all_gather | solution.py:40
  290.8 242.5 %copy-start.9 = (f32[64]{0:T(128)}, f32[64]{0:T(128)S(1)}, u32[]{:S(2)}) copy-start(f32[64]{0:T(128)S(1)} %div.49) | copy-start | bytes 772
  334.1 82.5 %copy-start.2 = (f32[64,768]{1,0:T(8,128)S(1)}, f32[64,768]{1,0:T(8,128)}, u32[]{:S(2)}) copy-start(f32[64,768]{1,0:T(8,128)} %multiply_add_fusion.6) | copy-start | bytes 589828
  334.1 335.7 %all-gather.12.cloned.1.call-start = ((), (), s32[]{:S(2)}) async-start(), calls=%async_computation.2 | async-start | bytes 6488064 | tf_op jit(solution)/shard_map/all_gather | solution.py:40
  533.3 214.8 %copy-start.13 = (f32[64]{0:T(128)}, f32[64]{0:T(128)S(1)}, u32[]{:S(2)}) copy-start(f32[64]{0:T(128)S(1)} %div.51) | copy-start | bytes 772
  575.8 94.0 %copy-start.4 = (f32[64,768]{1,0:T(8,128)S(1)}, f32[64,768]{1,0:T(8,128)}, u32[]{:S(2)}) copy-start(f32[64,768]{1,0:T(8,128)} %multiply_add_fusion.5) | copy-start | bytes 589828
  575.9 336.1 %all-gather.14.cloned.1.call-start = ((), (), s32[]{:S(2)}) async-start(), calls=%async_computation.3 | async-start | bytes 6488064 | tf_op jit(solution)/shard_map/all_gather | solution.py:40
  786.5 203.7 %copy-start.11 = (f32[64]{0:T(128)}, f32[64]{0:T(128)S(1)}, u32[]{:S(2)}) copy-start(f32[64]{0:T(128)S(1)} %div.53) | copy-start | bytes 772
  829.0 82.9 %copy-start.6 = (f32[64,768]{1,0:T(8,128)S(1)}, f32[64,768]{1,0:T(8,128)}, u32[]{:S(2)}) copy-start(f32[64,768]{1,0:T(8,128)} %multiply_add_fusion.4) | copy-start | bytes 589828
  829.0 324.8 %all-gather.16.cloned.1.call-start = ((), (), s32[]{:S(2)}) async-start(), calls=%async_computation.4 | async-start | bytes 6488064 | tf_op jit(solution)/shard_map/all_gather | solution.py:40
  1071.2 82.7 %copy-start.7 = (f32[64,768]{1,0:T(8,128)S(1)}, f32[64,768]{1,0:T(8,128)}, u32[]{:S(2)}) copy-start(f32[64,768]{1,0:T(8,128)} %multiply_add_fusion.3) | copy-start | bytes 589828
  1071.2 324.6 %all-gather.18.cloned.1.call-start = ((), (), s32[]{:S(2)}) async-start(), calls=%async_computation.5 | async-start | bytes 6488064 | tf_op jit(solution)/shard_map/all_gather | solution.py:40
  1313.3 82.5 %copy-start.8 = (f32[64,768]{1,0:T(8,128)S(1)}, f32[64,768]{1,0:T(8,128)}, u32[]{:S(2)}) copy-start(f32[64,768]{1,0:T(8,128)} %multiply_add_fusion.2) | copy-start | bytes 589828
  1395.7 117.1 %copy-start.1 = (f32[64,768]{1,0:T(8,128)S(1)}, f32[64,768]{1,0:T(8,128)}, u32[]{:S(2)}) copy-start(f32[64,768]{1,0:T(8,128)} %param.7) | copy-start | bytes 589828
  1395.7 117.1 %copy-start.3 = (f32[64,768]{1,0:T(8,128)S(1)}, f32[64,768]{1,0:T(8,128)}, u32[]{:S(2)}) copy-start(f32[64,768]{1,0:T(8,128)} %multiply_add_fusion.6) | copy-start | bytes 589828
  1395.7 117.1 %copy-start.5 = (f32[64,768]{1,0:T(8,128)S(1)}, f32[64,768]{1,0:T(8,128)}, u32[]{:S(2)}) copy-start(f32[64,768]{1,0:T(8,128)} %multiply_add_fusion.5) | copy-start | bytes 589828
  1395.7 117.1 %copy-start.10 = (f32[64]{0:T(128)S(1)}, f32[64]{0:T(128)}, u32[]{:S(2)}) copy-start(f32[64]{0:T(128)} %copy-done.9) | copy-start | bytes 772
  1395.7 117.1 %copy-start.12 = (f32[64]{0:T(128)S(1)}, f32[64]{0:T(128)}, u32[]{:S(2)}) copy-start(f32[64]{0:T(128)} %copy-done.11) | copy-start | bytes 772
  1395.8 117.1 %copy-start.14 = (f32[64]{0:T(128)S(1)}, f32[64]{0:T(128)}, u32[]{:S(2)}) copy-start(f32[64]{0:T(128)} %copy-done.13) | copy-start | bytes 772
Sparse Core Ops, SparseCore 0:
  10.9 72.5 all-gather.7
  334.3 68.3 all-gather.9
  576.0 68.3 all-gather.11
  829.2 68.5 all-gather.13
  1071.3 68.5 all-gather.15
  1313.4 68.6 all-gather.17
where the time goes:
time: 1530 us; the launch traced here: 1520 us
  blocking collectives  521 us (34%)
  other arithmetic  513 us (34%)
  matrix products  470 us (31%)
    reduce_sum x6, other arithmetic, local(): bending = lax.psum(jnp.sum(search * mapped, axis=1), ('row', 'col'))  507 us
    dot_general x6, matrix products, local(): lax.dot_general(lax.all_gather(search, ('row', 'col'), axis=1, tiled=True...  470 us
    psum x6, blocking collectives, squared_norm(): return lax.psum(jnp.sum(residual * residual, axis=1), ('row', 'col'))  246 us
    psum x5, blocking collectives, local(): bending = lax.psum(jnp.sum(search * mapped, axis=1), ('row', 'col'))  192 us
    all_gather x1, blocking collectives, local(): lax.all_gather(positions, ('row', 'col'), axis=1, tiled=True)  44.8 us
    all_gather x1, blocking collectives, local(): lax.all_gather(widths, ('row', 'col'), axis=0, tiled=True)  37.7 us
  transfers between devices with their start and end apart: 6, of which 0 were waited for; matrix products, arithmetic and copies ran while one was open for 33% of the time, Pallas kernels for 0%

commit v1 on v0

--- a/solution.py
+++ b/solution.py
@@ -6,6 +6,12 @@
 ITERS = 6
 root_two = 1.4142135623730951
 sqrt_pi = 1.7724538509055159
+
+
+def supply_core(local_array):
+    for no in ("col", "row"):
+        local_array = lax.psum(local_array, axis_name=no)
+    return local_array
 
 
 def kernel_block(pos_a, wid_a, pos_b, wid_b):
@@ -44,7 +50,7 @@
             preferred_element_type=jnp.float32,
         )
         mapped = summed + diagonal[None, :] * search
-        bending = lax.psum(jnp.sum(search * mapped, axis=1), ("row", "col"))
+        bending = supply_core(jnp.sum(search * mapped, axis=1))
         step_len = norm_now / bending
         charges = charges + step_len[:, None] * search
         residual = residual - step_len[:, None] * mapped

time: 1530 us -> 1480 us (0.967)
  blocking collectives: 521 us -> 465 us
    psum x5 -> x12, blocking collectives: 192 us -> 161 us  [supply_core(): local_array = lax.psum(local_array, axis_name=no)]
    psum x6, blocking collectives: 246 us -> 222 us  [squared_norm(): return lax.psum(jnp.sum(residual * residual, axis=1), ('row', 'col'))]
  transfers between devices with their start and end apart: 6 -> 6, of which waited for: 0 -> 0; matrix products, arithmetic and copies ran while one was open for 33% -> 35% of each run, Pallas kernels for 0% -> 0%
where the time goes in v1:
time: 1480 us; the launch traced here: 1460 us
  other arithmetic  513 us (35%)
  matrix products  470 us (32%)
  blocking collectives  465 us (31%)
    reduce_sum x6, other arithmetic, local(): bending = supply_core(jnp.sum(search * mapped, axis=1))  506 us
    dot_general x6, matrix products, local(): lax.dot_general(lax.all_gather(search, ('row', 'col'), axis=1, tiled=True...  470 us
    psum x6, blocking collectives, squared_norm(): return lax.psum(jnp.sum(residual * residual, axis=1), ('row', 'col'))  222 us
    psum x12, blocking collectives, supply_core(): local_array = lax.psum(local_array, axis_name=no)  161 us
    all_gather x1, blocking collectives, local(): lax.all_gather(positions, ('row', 'col'), axis=1, tiled=True)  44.8 us
    all_gather x1, blocking collectives, local(): lax.all_gather(widths, ('row', 'col'), axis=0, tiled=True)  37.7 us
  transfers between devices with their start and end apart: 6, of which 0 were waited for; matrix products, arithmetic and copies ran while one was open for 35% of the time, Pallas kernels for 0%

profile of v1, /device:TPU:0, one launch (start us, length us, event | category | flops | bytes accessed | tf_op | source)
XLA Modules:
  0.0 1464.9 jit_solution(10840282744595650860)
XLA Ops:
  7.2 0.0 copy-start
  7.2 0.0 all-gather.8.cloned.1.call-start
  7.2 0.7 all-gather.8.cloned.1.call-update
  7.9 0.0 all-gather.10.cloned.1.call-start
  8.0 44.8 %all_gather.24 = f32[3,24576]{1,0:T(4,128)S(1)} all-gather(f32[3,768]{1,0:T(4,128)} %param.4), channel_id=1, replica_groups=mesh['row'=8,'col'=4] {'row','col'}, dimensions={1}, use_global_device_ids=true | all-gather | bytes 304128 | tf_op jit(solution)/shard_map/all_gather | solution.py:36
  52.8 0.8 slice_reduce_fusion.2
  53.6 0.2 fusion.53
  53.9 0.7 reshape.23
  54.5 0.7 divide_add_fusion
  55.3 37.7 %all-gather = f32[32,1,768]{2,1,0:T(1,128)S(1)} all-gather(f32[1,1,768]{2,1,0:T(1,128)S(1)} %reshape.23), channel_id=1, replica_groups=mesh['row'=8,'col'=4] {'row','col'}, dimensions={0}, use_global_device_ids=true | all-gather | bytes 101376 | tf_op jit(solution)/shard_map/all_gather | solution.py:37
  93.0 0.1 mul.283
  93.1 82.4 %fusion.19.clone.4 = f32[768,24576]{1,0:T(8,128)} fusion(f32[24576]{0:T(1024)S(1)} %bitcast.40, f32[768]{0:T(1024)S(1)} %get-tuple-element.19, f32[24576]{0:T(1024)S(1)} %bitcast.28, f32[768]{0:T(1024)S(1)} %get-tuple-element.5, f32[24576]{0:T(1024)S(1)} %bitcast.34, f32[768]{0:T(1024)S(1)} %get-tuple-element.6, ...), kind=kLoop, calls=%fused_computation.1.clone.5.clone.clone.clone.clone.clone.clone.clone.1 | loop fusion | flops 283115520 | bytes 75902976 | tf_op jit(solution)/shard_map/reduce_sum | solution.py:53
  175.5 78.1 %multiply_reduce_fusion.10 = (f32[64]{0:T(128)S(1)}, f32[64]{0:T(128)S(1)}, f32[64,768]{1,0:T(8,128)S(1)}) fusion(f32[64,768]{1,0:T(8,128)S(1)} %copy-done, f32[768]{0:T(1024)S(1)} %get-tuple-element.18, f32[64,24576]{1,0:T(8,128)} %all-gather.8.cloned.1.call-done, f32[768,24576]{1,0:T(8,128)} %fusion.19.clone.4), kind=kOutput, calls=%fused_computation.39 | convolution fusion | flops 14495809536 | bytes 82185728 | tf_op jit(solution)/shard_map/dot_general | solution.py:45
  253.7 37.1 %psum.126 = f32[64]{0:T(128)S(1)} all-reduce(f32[64]{0:T(128)S(1)} %get-tuple-element.3), channel_id=1, replica_groups=mesh['row'=8,'col'=4] {'row','col'}, use_global_device_ids=true, to_apply=%region_1.2 | all-reduce | flops 64 | bytes 512 | tf_op jit(solution)/shard_map/psum | solution.py:30
  290.8 6.6 psum.127
  297.4 20.1 %psum.128 = f32[64]{0:T(128)S(1)} all-reduce(f32[64]{0:T(128)S(1)} %psum.127), channel_id=1, replica_groups=mesh['row'=8,'col'=4] {'row'}, use_global_device_ids=true, to_apply=%region_4.5 | all-reduce | flops 64 | bytes 512 | tf_op jit(solution)/shard_map/psum | solution.py:13
  317.5 0.2 multiply_reduce_fusion.9
  317.7 36.9 %psum.129 = f32[64]{0:T(128)S(1)} all-reduce(f32[64]{0:T(128)S(1)} %multiply_reduce_fusion.9), channel_id=1, replica_groups=mesh['row'=8,'col'=4] {'row','col'}, use_global_device_ids=true, to_apply=%region_6.7 | all-reduce | flops 64 | bytes 512 | tf_op jit(solution)/shard_map/psum | solution.py:30
  354.6 0.8 multiply_add_fusion.6
  355.4 0.0 all-gather.10.cloned.1.call-update
  355.4 0.0 all-gather.12.cloned.1.call-start
  355.4 82.4 %fusion.22.clone.2 = f32[768,24576]{1,0:T(8,128)} fusion(f32[24576]{0:T(1024)S(1)} %bitcast.41, f32[768]{0:T(1024)S(1)} %get-tuple-element.19, f32[24576]{0:T(1024)S(1)} %bitcast.29, f32[768]{0:T(1024)S(1)} %get-tuple-element.5, f32[24576]{0:T(1024)S(1)} %bitcast.35, f32[768]{0:T(1024)S(1)} %get-tuple-element.6, ...), kind=kLoop, calls=%fused_computation.1.clone.4.clone.clone.clone.clone.clone | loop fusion | flops 283115520 | bytes 75902976 | tf_op jit(solution)/shard_map/reduce_sum | solution.py:53
  437.9 78.3 %multiply_reduce_fusion.8 = (f32[64]{0:T(128)S(1)}, f32[64,768]{1,0:T(8,128)S(1)}) fusion(f32[64,768]{1,0:T(8,128)S(1)} %copy-done.2, f32[768]{0:T(1024)S(1)} %get-tuple-element.18, f32[64,24576]{1,0:T(8,128)} %all-gather.10.cloned.1.call-done, f32[768,24576]{1,0:T(8,128)} %fusion.22.clone.2), kind=kOutput, calls=%fused_computation.35 | convolution fusion | flops 14495711232 | bytes 82185472 | tf_op jit(solution)/shard_map/dot_general | solution.py:45
  516.2 6.8 psum.130
  523.0 19.9 %psum.131 = f32[64]{0:T(128)S(1)} all-reduce(f32[64]{0:T(128)S(1)} %psum.130), channel_id=1, replica_groups=mesh['row'=8,'col'=4] {'row'}, use_global_device_ids=true, to_apply=%region_9.10 | all-reduce | flops 64 | bytes 512 | tf_op jit(solution)/shard_map/psum | solution.py:13
  542.9 0.2 multiply_reduce_fusion.7
  543.1 36.8 %psum.132 = f32[64]{0:T(128)S(1)} all-reduce(f32[64]{0:T(128)S(1)} %get-tuple-element.13), channel_id=1, replica_groups=mesh['row'=8,'col'=4] {'row','col'}, use_global_device_ids=true, to_apply=%region_11.12 | all-reduce | flops 64 | bytes 512 | tf_op jit(solution)/shard_map/psum | solution.py:30
  580.0 0.8 multiply_add_fusion.5
  580.8 0.0 all-gather.12.cloned.1.call-update
  580.8 0.0 all-gather.14.cloned.1.call-start
  580.8 93.6 %fusion.25.clone.2 = f32[768,24576]{1,0:T(8,128)} fusion(f32[24576]{0:T(1024)S(1)} %bitcast.42, f32[768]{0:T(1024)S(1)} %get-tuple-element.19, f32[24576]{0:T(1024)S(1)} %bitcast.30, f32[768]{0:T(1024)S(1)} %get-tuple-element.5, f32[24576]{0:T(1024)S(1)} %bitcast.36, f32[768]{0:T(1024)S(1)} %get-tuple-element.6, ...), kind=kLoop, calls=%fused_computation.1.clone.3.clone.clone.clone.clone.clone | loop fusion | flops 283115520 | bytes 75902976 | tf_op jit(solution)/shard_map/reduce_sum | solution.py:53
  674.4 78.3 %multiply_reduce_fusion.6 = (f32[64]{0:T(128)S(1)}, f32[64,768]{1,0:T(8,128)S(1)}) fusion(f32[64,768]{1,0:T(8,128)S(1)} %copy-done.4, f32[768]{0:T(1024)S(1)} %get-tuple-element.18, f32[64,24576]{1,0:T(8,128)} %all-gather.12.cloned.1.call-done, f32[768,24576]{1,0:T(8,128)} %fusion.25.clone.2), kind=kOutput, calls=%fused_computation.31 | convolution fusion | flops 14495711232 | bytes 82185472 | tf_op jit(solution)/shard_map/dot_general | solution.py:45
  752.7 7.0 psum.133
  759.6 19.8 %psum.134 = f32[64]{0:T(128)S(1)} all-reduce(f32[64]{0:T(128)S(1)} %psum.133), channel_id=1, replica_groups=mesh['row'=8,'col'=4] {'row'}, use_global_device_ids=true, to_apply=%region_14.15 | all-reduce | flops 64 | bytes 512 | tf_op jit(solution)/shard_map/psum | solution.py:13
  779.5 0.2 multiply_reduce_fusion.5
  779.7 36.9 %psum.135 = f32[64]{0:T(128)S(1)} all-reduce(f32[64]{0:T(128)S(1)} %get-tuple-element.11), channel_id=1, replica_groups=mesh['row'=8,'col'=4] {'row','col'}, use_global_device_ids=true, to_apply=%region_16.17 | all-reduce | flops 64 | bytes 512 | tf_op jit(solution)/shard_map/psum | solution.py:30
  816.5 0.8 multiply_add_fusion.4
  817.3 0.0 all-gather.14.cloned.1.call-update
  817.3 0.0 all-gather.16.cloned.1.call-start
  817.4 82.8 %fusion.28.clone.2 = f32[768,24576]{1,0:T(8,128)} fusion(f32[24576]{0:T(1024)S(1)} %bitcast.43, f32[768]{0:T(1024)S(1)} %get-tuple-element.19, f32[24576]{0:T(1024)S(1)} %bitcast.31, f32[768]{0:T(1024)S(1)} %get-tuple-element.5, f32[24576]{0:T(1024)S(1)} %bitcast.37, f32[768]{0:T(1024)S(1)} %get-tuple-element.6, ...), kind=kLoop, calls=%fused_computation.1.clone.2.clone.clone.clone.clone.clone | loop fusion | flops 283115520 | bytes 75902976 | tf_op jit(solution)/shard_map/reduce_sum | solution.py:53
  900.2 78.3 %multiply_reduce_fusion.4 = (f32[64]{0:T(128)S(1)}, f32[64,768]{1,0:T(8,128)S(1)}) fusion(f32[64,768]{1,0:T(8,128)S(1)} %copy-done.6, f32[768]{0:T(1024)S(1)} %get-tuple-element.18, f32[64,24576]{1,0:T(8,128)} %all-gather.14.cloned.1.call-done, f32[768,24576]{1,0:T(8,128)} %fusion.28.clone.2), kind=kOutput, calls=%fused_computation.27 | convolution fusion | flops 14495711232 | bytes 82185472 | tf_op jit(solution)/shard_map/dot_general | solution.py:45
  978.5 7.0 psum.136
  985.5 19.8 %psum.137 = f32[64]{0:T(128)S(1)} all-reduce(f32[64]{0:T(128)S(1)} %psum.136), channel_id=1, replica_groups=mesh['row'=8,'col'=4] {'row'}, use_global_device_ids=true, to_apply=%region_19.20 | all-reduce | flops 64 | bytes 512 | tf_op jit(solution)/shard_map/psum | solution.py:13
  1005.3 0.2 multiply_reduce_fusion.3
  1005.5 36.9 %psum.138 = f32[64]{0:T(128)S(1)} all-reduce(f32[64]{0:T(128)S(1)} %get-tuple-element.9), channel_id=1, replica_groups=mesh['row'=8,'col'=4] {'row','col'}, use_global_device_ids=true, to_apply=%region_21.22 | all-reduce | flops 64 | bytes 512 | tf_op jit(solution)/shard_map/psum | solution.py:30
  1042.4 0.8 multiply_add_fusion.3
  1043.2 0.0 all-gather.16.cloned.1.call-update
  1043.2 0.0 all-gather.18.cloned.1.call-start
  1043.3 82.6 %fusion.31.clone.2 = f32[768,24576]{1,0:T(8,128)} fusion(f32[24576]{0:T(1024)S(1)} %bitcast.44, f32[768]{0:T(1024)S(1)} %get-tuple-element.19, f32[24576]{0:T(1024)S(1)} %bitcast.32, f32[768]{0:T(1024)S(1)} %get-tuple-element.5, f32[24576]{0:T(1024)S(1)} %bitcast.38, f32[768]{0:T(1024)S(1)} %get-tuple-element.6, ...), kind=kLoop, calls=%fused_computation.1.clone.1.clone.clone.clone.clone.clone | loop fusion | flops 283115520 | bytes 75902976 | tf_op jit(solution)/shard_map/reduce_sum | solution.py:53
  1125.9 78.3 %multiply_reduce_fusion.2 = (f32[64]{0:T(128)S(1)}, f32[64,768]{1,0:T(8,128)S(1)}) fusion(f32[64,768]{1,0:T(8,128)S(1)} %copy-done.7, f32[768]{0:T(1024)S(1)} %get-tuple-element.18, f32[64,24576]{1,0:T(8,128)} %all-gather.16.cloned.1.call-done, f32[768,24576]{1,0:T(8,128)} %fusion.31.clone.2), kind=kOutput, calls=%fused_computation.23 | convolution fusion | flops 14495711232 | bytes 82185472 | tf_op jit(solution)/shard_map/dot_general | solution.py:45
  1204.2 7.1 psum.139
  1211.2 19.7 %psum.140 = f32[64]{0:T(128)S(1)} all-reduce(f32[64]{0:T(128)S(1)} %psum.139), channel_id=1, replica_groups=mesh['row'=8,'col'=4] {'row'}, use_global_device_ids=true, to_apply=%region_24.25 | all-reduce | flops 64 | bytes 512 | tf_op jit(solution)/shard_map/psum | solution.py:13
  1230.9 0.2 multiply_reduce_fusion.1
  1231.1 37.1 %psum.141 = f32[64]{0:T(128)S(1)} all-reduce(f32[64]{0:T(128)S(1)} %get-tuple-element.7), channel_id=1, replica_groups=mesh['row'=8,'col'=4] {'row','col'}, use_global_device_ids=true, to_apply=%region_26.27 | all-reduce | flops 64 | bytes 512 | tf_op jit(solution)/shard_map/psum | solution.py:30
  1268.2 0.8 multiply_add_fusion.2
  1269.0 0.0 all-gather.18.cloned.1.call-update
  1269.0 82.4 %fusion.34.clone.4 = f32[768,24576]{1,0:T(8,128)} fusion(f32[24576]{0:T(1024)S(1)} %bitcast.45, f32[768]{0:T(1024)S(1)} %get-tuple-element.19, f32[24576]{0:T(1024)S(1)} %bitcast.33, f32[768]{0:T(1024)S(1)} %get-tuple-element.5, f32[24576]{0:T(1024)S(1)} %bitcast.39, f32[768]{0:T(1024)S(1)} %get-tuple-element.6, ...), kind=kLoop, calls=%fused_computation.1.clone.clone.clone.clone.clone.clone.1 | loop fusion | flops 283115520 | bytes 75902976 | tf_op jit(solution)/shard_map/reduce_sum | solution.py:53
  1351.5 0.0 copy-start.10
  1351.5 0.0 copy-start.12
  1351.5 0.0 all-gather.18.cloned.1.call-done
  1351.6 78.4 %multiply_reduce_fusion = (f32[64]{0:T(128)S(1)}, f32[64,768]{1,0:T(8,128)S(1)}) fusion(f32[64,768]{1,0:T(8,128)S(1)} %copy-done.8, f32[768]{0:T(1024)S(1)} %get-tuple-element.18, f32[64,24576]{1,0:T(8,128)} %all-gather.18.cloned.1.call-done, f32[768,24576]{1,0:T(8,128)} %fusion.34.clone.4), kind=kOutput, calls=%fused_computation.19 | convolution fusion | flops 14495711232 | bytes 82185472 | tf_op jit(solution)/shard_map/dot_general | solution.py:45
  1430.0 7.1 psum.142
  1437.0 19.7 %psum.143 = f32[64]{0:T(128)S(1)} all-reduce(f32[64]{0:T(128)S(1)} %psum.142), channel_id=1, replica_groups=mesh['row'=8,'col'=4] {'row'}, use_global_device_ids=true, to_apply=%region_29.30 | all-reduce | flops 64 | bytes 512 | tf_op jit(solution)/shard_map/psum | solution.py:13
  1456.8 0.9 multiply_subtract_fusion
  (43 shorter events, 0.1 us)
Async XLA Ops:
  7.2 168.3 %copy-start = (f32[64,768]{1,0:T(8,128)S(1)}, f32[64,768]{1,0:T(8,128)}, u32[]{:S(2)}) copy-start(f32[64,768]{1,0:T(8,128)} %param.7) | copy-start | bytes 589828
  7.2 168.3 %all-gather.8.cloned.1.call-start = ((), (), s32[]{:S(2)}) async-start(), calls=%async_computation | async-start | bytes 6488064 | tf_op jit(solution)/shard_map/all_gather | solution.py:46
  7.9 430.0 %all-gather.10.cloned.1.call-start = ((), (), s32[]{:S(2)}) async-start(), calls=%async_computation.1 | async-start | bytes 6488064 | tf_op jit(solution)/shard_map/all_gather | solution.py:46
  317.5 225.4 %copy-start.9 = (f32[64]{0:T(128)}, f32[64]{0:T(128)S(1)}, u32[]{:S(2)}) copy-start(f32[64]{0:T(128)S(1)} %div.49) | copy-start | bytes 772
  355.4 82.5 %copy-start.2 = (f32[64,768]{1,0:T(8,128)S(1)}, f32[64,768]{1,0:T(8,128)}, u32[]{:S(2)}) copy-start(f32[64,768]{1,0:T(8,128)} %multiply_add_fusion.6) | copy-start | bytes 589828
  355.4 319.0 %all-gather.12.cloned.1.call-start = ((), (), s32[]{:S(2)}) async-start(), calls=%async_computation.2 | async-start | bytes 6488064 | tf_op jit(solution)/shard_map/all_gather | solution.py:46
  542.9 209.7 %copy-start.13 = (f32[64]{0:T(128)}, f32[64]{0:T(128)S(1)}, u32[]{:S(2)}) copy-start(f32[64]{0:T(128)S(1)} %div.51) | copy-start | bytes 772
  580.7 93.6 %copy-start.4 = (f32[64,768]{1,0:T(8,128)S(1)}, f32[64,768]{1,0:T(8,128)}, u32[]{:S(2)}) copy-start(f32[64,768]{1,0:T(8,128)} %multiply_add_fusion.5) | copy-start | bytes 589828
  580.8 319.4 %all-gather.14.cloned.1.call-start = ((), (), s32[]{:S(2)}) async-start(), calls=%async_computation.3 | async-start | bytes 6488064 | tf_op jit(solution)/shard_map/all_gather | solution.py:46
  779.5 199.1 %copy-start.11 = (f32[64]{0:T(128)}, f32[64]{0:T(128)S(1)}, u32[]{:S(2)}) copy-start(f32[64]{0:T(128)S(1)} %div.53) | copy-start | bytes 772
  817.3 82.9 %copy-start.6 = (f32[64,768]{1,0:T(8,128)S(1)}, f32[64,768]{1,0:T(8,128)}, u32[]{:S(2)}) copy-start(f32[64,768]{1,0:T(8,128)} %multiply_add_fusion.4) | copy-start | bytes 589828
  817.3 308.5 %all-gather.16.cloned.1.call-start = ((), (), s32[]{:S(2)}) async-start(), calls=%async_computation.4 | async-start | bytes 6488064 | tf_op jit(solution)/shard_map/all_gather | solution.py:46
  1043.2 82.7 %copy-start.7 = (f32[64,768]{1,0:T(8,128)S(1)}, f32[64,768]{1,0:T(8,128)}, u32[]{:S(2)}) copy-start(f32[64,768]{1,0:T(8,128)} %multiply_add_fusion.3) | copy-start | bytes 589828
  1043.2 308.3 %all-gather.18.cloned.1.call-start = ((), (), s32[]{:S(2)}) async-start(), calls=%async_computation.5 | async-start | bytes 6488064 | tf_op jit(solution)/shard_map/all_gather | solution.py:46
  1269.0 82.5 %copy-start.8 = (f32[64,768]{1,0:T(8,128)S(1)}, f32[64,768]{1,0:T(8,128)}, u32[]{:S(2)}) copy-start(f32[64,768]{1,0:T(8,128)} %multiply_add_fusion.2) | copy-start | bytes 589828
  1351.5 105.3 %copy-start.1 = (f32[64,768]{1,0:T(8,128)S(1)}, f32[64,768]{1,0:T(8,128)}, u32[]{:S(2)}) copy-start(f32[64,768]{1,0:T(8,128)} %param.7) | copy-start | bytes 589828
  1351.5 105.3 %copy-start.3 = (f32[64,768]{1,0:T(8,128)S(1)}, f32[64,768]{1,0:T(8,128)}, u32[]{:S(2)}) copy-start(f32[64,768]{1,0:T(8,128)} %multiply_add_fusion.6) | copy-start | bytes 589828
  1351.5 105.3 %copy-start.5 = (f32[64,768]{1,0:T(8,128)S(1)}, f32[64,768]{1,0:T(8,128)}, u32[]{:S(2)}) copy-start(f32[64,768]{1,0:T(8,128)} %multiply_add_fusion.5) | copy-start | bytes 589828
  1351.5 105.3 %copy-start.10 = (f32[64]{0:T(128)S(1)}, f32[64]{0:T(128)}, u32[]{:S(2)}) copy-start(f32[64]{0:T(128)} %copy-done.9) | copy-start | bytes 772
  1351.5 105.3 %copy-start.12 = (f32[64]{0:T(128)S(1)}, f32[64]{0:T(128)}, u32[]{:S(2)}) copy-start(f32[64]{0:T(128)} %copy-done.11) | copy-start | bytes 772
  1351.5 105.3 %copy-start.14 = (f32[64]{0:T(128)S(1)}, f32[64]{0:T(128)}, u32[]{:S(2)}) copy-start(f32[64]{0:T(128)} %copy-done.13) | copy-start | bytes 772
Sparse Core Ops, SparseCore 0:
  10.9 72.5 all-gather.7
  355.5 70.8 all-gather.9
  580.9 71.0 all-gather.11
  817.5 71.0 all-gather.13
  1043.3 71.1 all-gather.15
  1269.2 71.1 all-gather.17
